TPU v7x, 32 devices: a whole 2x2x4 slice. The times are simulated.
32 devices in a mesh: ty: 4 (over x, core), tx: 8 (over z, y).
Axes of the slice: x: 2, y: 2, z: 4, core: 2. Of those that a mesh axis runs over, the one named last changes fastest.
Arguments:
- exposures: float32 [256, 128, 128], P(('ty', 'tx')), may hold values from -70 to 70
- point_spread: float32 [256, 31, 31], P(('ty', 'tx')), may hold values from 0.0001 to 1
- warp_steps: int32 [256, 2], P(('ty', 'tx')), may hold values from 0 to 3
- column: int32 [256, 1], P(('ty', 'tx')), may hold values from 0 to 7; in each aligned block of 8 rows (0 to 7, 8 to 15, ...) at most 2 rows name the same one
- block_cell: int32 [256], P(('ty', 'tx')), may hold values from 0 to 15
Outputs:
- solution: float32 [2048, 4096], P('ty', 'tx')
- residual: float32 [2048, 4096], P('ty', 'tx')
Inputs may be any that keep to these rules, and one draw needn't show every extreme that they name: `column`: among the 8 frame blocks of one device (aligned blocks of 8 rows) no value occurs more than 2 times, and in some such block one value occurs exactly 2 times.
All inputs are finite; a program needn't handle non-finite values.
Results may differ from a plain program's by a relative error of at most 0.0042.
Values may be sent and summed in bfloat16 or wider, within the bound.
A program may use at most 192 MiB of HBM per device.

v0:
```python
import jax
import jax.numpy as jnp
from jax import lax
from jax.sharding import PartitionSpec as P

TILE = 512
SUB = 4
ITERS = 2


damping = 0.05


def with_halo(value, sides, width):
    for axis, dim in sides:
        size, length = (lax.axis_size(axis), value.shape[dim])
        up = [(i, (i + 1) % size) for i in range(size - 1)]
        down = [(j, i) for i, j in up]
        last = lax.slice_in_dim(value, length - width, length, axis=dim)
        first = lax.slice_in_dim(value, 0, width, axis=dim)
        before = lax.ppermute(last, axis, up)
        after = lax.ppermute(first, axis, down)
        value = jnp.concatenate([before, value, after], axis=dim)
    return value


def make_kernels(point_spread, warp_steps):
    tap_count = point_spread.shape[-1] + 1
    totals = jnp.sum(point_spread, axis=(1, 2), keepdims=True)
    padded = jnp.pad(point_spread / totals, ((0, 0), (0, 1), (0, 1)))
    row_frac = (warp_steps[:, 0].astype(jnp.float32) / SUB)[:, None, None]
    col_frac = (warp_steps[:, 1].astype(jnp.float32) / SUB)[:, None, None]
    shifted = jnp.pad(padded, ((0, 0), (0, 0), (1, 0)))[:, :, :tap_count]
    blended = (1.0 - col_frac) * padded + col_frac * shifted
    lowered = jnp.pad(blended, ((0, 0), (1, 0), (0, 0)))[:, :tap_count, :]
    return ((1.0 - row_frac) * blended + row_frac * lowered).astype(jnp.bfloat16)


def tap_table(tap_count, block_side, window):
    taps_index = jnp.arange(tap_count)[:, None, None]
    positions = jnp.arange(window)[:, None]
    columns = jnp.arange(block_side)[None, :]
    forward_table = jnp.where(positions - columns == taps_index, 1.0, 0.0).astype(jnp.bfloat16)
    return forward_table.reshape(tap_count, window * block_side)


def build_bands(kernels, forward_table, block_side, window, tap_count):

    def one_band(kernel):
        banded = jnp.dot(kernel, forward_table, preferred_element_type=jnp.float32).astype(
            jnp.bfloat16
        )
        return banded.reshape(tap_count * window, block_side)

    return lax.map(one_band, kernels)


def forward_block(flat_window, banded, block_side, window, tap_count):
    framed = flat_window.reshape(window, window)
    stacked = jnp.concatenate(
        [framed[offset : offset + block_side] for offset in range(tap_count)], axis=1
    )
    return jnp.dot(stacked, banded, preferred_element_type=jnp.float32)


def adjoint_block(frame_image, banded, block_side, window, tap_count):
    spread = lax.dot_general(
        frame_image, banded, (((1,), (1,)), ((), ())), preferred_element_type=jnp.float32
    )
    spread = spread.reshape(block_side, tap_count, window)
    summed = jnp.zeros((window, window), jnp.float32)
    for offset in range(tap_count):
        summed = summed + jnp.pad(
            spread[:, offset, :], ((offset, window - block_side - offset), (0, 0))
        )
    return summed


def split_rows(values, block_side, margin, count):
    head = values[: count * block_side].reshape(count, block_side, -1)
    tail = jnp.pad(values[block_side:], ((0, block_side - 2 * margin), (0, 0)))
    tail = tail.reshape(count, block_side, -1)[:, : 2 * margin]
    return jnp.concatenate([head, tail], axis=1)


def fold_rows(pieces, block_side, margin, count):
    extent = count * block_side + 2 * margin
    head = pieces[:, :block_side].reshape(count * block_side, -1)
    tail = jnp.pad(pieces[:, block_side:], ((0, 0), (0, block_side - 2 * margin), (0, 0))).reshape(
        count * block_side, -1
    )
    return (
        jnp.pad(head, ((0, 2 * margin), (0, 0))) + jnp.pad(tail, ((block_side, 0), (0, 0)))[:extent]
    )


def fold_edges(values, axis_index, margin, extent):
    interior = lax.slice_in_dim(values, 2 * margin, 2 * margin + extent, axis=axis_index)
    lower_rim = lax.slice_in_dim(values, 0, margin, axis=axis_index)
    upper_rim = lax.slice_in_dim(values, extent + 3 * margin, extent + 4 * margin, axis=axis_index)
    widths_low = [(0, 0)] * values.ndim
    widths_high = [(0, 0)] * values.ndim
    widths_low[axis_index] = (0, extent - margin)
    widths_high[axis_index] = (extent - margin, 0)
    return interior + jnp.pad(lower_rim, widths_low) + jnp.pad(upper_rim, widths_high)


def body(exposures, point_spread, warp_steps, column, block_cell):
    frame_count = exposures.shape[0]
    block_side = exposures.shape[1]
    tap_count = point_spread.shape[1] + 1
    margin = tap_count // 2
    window = block_side + 2 * margin
    tx_size = lax.axis_size("tx")
    capacity = max(2, 2 * frame_count // tx_size)
    slot_count = tx_size * capacity
    per_row = TILE // block_side
    cell_count = per_row * per_row
    extent = TILE + 2 * margin
    kernels = make_kernels(point_spread, warp_steps)
    forward_table = tap_table(tap_count, block_side, window)
    target = column[:, 0]
    earlier = jnp.arange(frame_count)[:, None] > jnp.arange(frame_count)[None, :]
    matching = target[:, None] == target[None, :]
    standing = jnp.sum(jnp.where(earlier & matching, 1, 0), axis=1)
    slot_index = target * capacity + standing
    chosen = jnp.where(slot_index[None, :] == jnp.arange(slot_count)[:, None], 1, 0).astype(
        jnp.int32
    )
    chosen_low = chosen.astype(jnp.bfloat16)
    chosen_wide = chosen.astype(jnp.float32)
    request = jnp.sum(chosen * (block_cell + 1)[None, :], axis=1).reshape(tx_size, capacity)
    incoming = lax.all_to_all(request, "tx", split_axis=0, concat_axis=0, tiled=True)
    wanted_cell = incoming.reshape(slot_count) - 1
    picking = wanted_cell[:, None] == jnp.arange(cell_count)[None, :]
    pick_low = jnp.where(picking, 1.0, 0.0).astype(jnp.bfloat16)
    pick_wide = jnp.where(picking, 1.0, 0.0).astype(jnp.float32)

    def spread_back(patches):
        cell_sums = jnp.dot(pick_wide.T, patches, precision=lax.Precision.HIGHEST)
        arranged = (
            cell_sums.reshape(per_row, per_row, window, window)
            .transpose(0, 2, 1, 3)
            .reshape(per_row, window, per_row * window)
        )
        row_folded = fold_rows(arranged, block_side, margin, per_row)
        turned = row_folded.reshape(extent, per_row, window).transpose(1, 2, 0)
        accumulated = fold_rows(turned, block_side, margin, per_row).T
        extended = with_halo(accumulated, (("ty", 0), ("tx", 1)), margin)
        return fold_edges(fold_edges(extended, 0, margin, TILE), 1, margin, TILE)

    def apply_forward(operands):
        return forward_block(operands[0], operands[1], block_side, window, tap_count)

    def apply_back(operands):
        return adjoint_block(operands[0], operands[1], block_side, window, tap_count)

    frame_bands = build_bands(kernels, forward_table, block_side, window, tap_count)

    def adjoint_pass(images_low):
        patches = lax.map(apply_back, (images_low, frame_bands)).reshape(frame_count, -1)
        outgoing = jnp.dot(chosen_wide, patches, precision=lax.Precision.HIGHEST)
        returned = lax.all_to_all(
            outgoing.reshape(tx_size, capacity, -1), "tx", split_axis=0, concat_axis=0, tiled=True
        )
        return spread_back(returned.reshape(slot_count, -1))

    first_images = exposures.astype(jnp.bfloat16)
    right_side = adjoint_pass(first_images)
    solution = jnp.zeros_like(right_side)
    residual = right_side
    direction = right_side
    norm_now = lax.psum(jnp.sum(residual * residual), ("ty", "tx"))
    for iteration in range(ITERS):
        cut_extended = with_halo(direction.astype(jnp.bfloat16), (("ty", 0), ("tx", 1)), margin)
        row_pieces = split_rows(cut_extended, block_side, margin, per_row)
        cut_turned = row_pieces.transpose(2, 0, 1).reshape(extent, per_row * window)
        both = split_rows(cut_turned, block_side, margin, per_row).reshape(
            per_row, window, per_row, window
        )
        cell_windows = both.transpose(2, 0, 3, 1).reshape(cell_count, window * window)
        pieces = (
            jnp.dot(pick_low, cell_windows, preferred_element_type=jnp.float32)
            .astype(jnp.bfloat16)
            .reshape(tx_size, capacity, -1)
        )
        arrived = lax.all_to_all(pieces, "tx", split_axis=0, concat_axis=0, tiled=True).reshape(
            slot_count, -1
        )
        own_windows = jnp.dot(chosen_low.T, arrived, preferred_element_type=jnp.float32).astype(
            jnp.bfloat16
        )
        modelled = lax.map(apply_forward, (own_windows, frame_bands))
        applied = adjoint_pass(modelled.astype(jnp.bfloat16)) + damping * direction
        curvature, cross_term, square = lax.psum(
            (jnp.sum(direction * applied), jnp.sum(residual * applied), jnp.sum(applied * applied)),
            ("ty", "tx"),
        )
        step_size = norm_now / curvature
        solution = solution + step_size * direction
        residual = residual - step_size * applied
        if iteration + 1 < ITERS:
            norm_next = norm_now - 2.0 * step_size * cross_term + step_size * step_size * square
            direction = residual + norm_next / norm_now * direction
            norm_now = norm_next
    return (solution, residual)


def solution(mesh):
    placed = (
        P(("ty", "tx"), None, None),
        P(("ty", "tx"), None, None),
        P(("ty", "tx"), None),
        P(("ty", "tx"), None),
        P(("ty", "tx")),
    )
    return jax.shard_map(
        body, mesh=mesh, in_specs=placed, out_specs=(P("ty", "tx"), P("ty", "tx")), check_vma=False
    )
```

profile of v0, /device:TPU:0, one launch (start us, length us, event | category | flops | bytes accessed | tf_op | source)
XLA Modules:
  0.0 1152.2 jit_solution(9350103348989374002)
XLA Ops:
  3.0 7.3 all-to-all-start
  14.2 18.6 %while.72 = (s32[]{:T(128)}, bf16[8,5120,128]{2,1,0:T(8,128)(2,1)}, bf16[8,32,32]{2,1,0:T(8,128)(2,1)S(1)}, s32[20480]{0:T(1024)S(1)}, s32[]{:T(128)}) while((s32[]{:T(128)}, bf16[8,5120,128]{2,1,0:T(8,128)(2,1)}, bf16[8,32,32]{2,1,0:T(8,128)(2,1)S(1)}, s32[20480]{0:T(1024)S(1)}, s32[]{:T(128)}) %tuple.303), condition=%wide.region_4.5_spmd.clone, body=%wide.region_3.4_spmd.clone.sunk | while | flops 44564480 | bytes 6644289 | solution.py:55
  32.9 29.3 %while.67 = (s32[]{:T(128)}, f32[8,160,160]{2,1,0:T(8,128)S(1)}, bf16[8,128,128]{2,1,0:T(8,128)(2,1)S(1)}, bf16[8,5120,128]{2,1,0:T(8,128)(2,1)}, s32[]{:T(128)}) while((s32[]{:T(128)}, f32[8,160,160]{2,1,0:T(8,128)S(1)}, bf16[8,128,128]{2,1,0:T(8,128)(2,1)S(1)}, bf16[8,5120,128]{2,1,0:T(8,128)(2,1)}, s32[]{:T(128)}) %tuple.306), condition=%wide.region_6.7_spmd, body=%wide.region_5.6_spmd.sunk | while | flops 168565760 | bytes 15085641 | solution.py:161
  67.0 6.3 all-to-all-start.1
  73.4 37.7 %all-to-all-done.1 = f32[8,2,25600]{2,1,0:T(2,128)S(1)} async-done(((f32[8,2,25600]{2,1,0:T(2,128)}), f32[8,2,25600]{2,1,0:T(2,128)S(1)}, u32[]{:S(2)}, u32[]{:S(2)}) %all-to-all-start.1) | async-done | bytes 1638432 | tf_op jit(solution)/shard_map/all_to_all | solution.py:163
  116.0 5.9 fusion.51
  137.7 3.5 collective-permute-done.1
  141.4 3.3 collective-permute-start.2
  146.1 10.6 collective-permute-done.2
  158.0 3.8 collective-permute-start.4
  164.9 4.1 collective-permute-start.6
  172.1 4.7 collective-permute-done.7
  186.1 5.0 all-to-all-start.2
  191.1 21.3 %all-to-all-done.2 = bf16[8,2,25600]{2,1,0:T(2,128)(2,1)S(1)} async-done(((bf16[8,2,25600]{2,1,0:T(2,128)(2,1)}), bf16[8,2,25600]{2,1,0:T(2,128)(2,1)S(1)}, u32[]{:S(2)}, u32[]{:S(2)}) %all-to-all-start.2) | async-done | bytes 819232 | tf_op jit(solution)/shard_map/all_to_all | solution.py:187
  213.8 251.8 %while.68 = (s32[]{:T(128)}, bf16[8,128,128]{2,1,0:T(8,128)(2,1)}, bf16[8,25600]{1,0:T(8,128)(2,1)S(1)}, bf16[8,5120,128]{2,1,0:T(8,128)(2,1)}, s32[]{:T(128)}, ...) while((s32[]{:T(128)}, bf16[8,128,128]{2,1,0:T(8,128)(2,1)}, ...), condition=%wide.region_10.11_spmd, body=%wide.region_9.10_spmd.sunk | while | flops 167772192 | bytes 10553141 | solution.py:193
  214.2 5.5 dynamic-slice_reduce_fusion.68
  225.7 4.1 dynamic-slice_reduce_fusion.69
  245.6 5.5 dynamic-slice_reduce_fusion.68
  257.1 4.1 dynamic-slice_reduce_fusion.69
  277.0 5.5 dynamic-slice_reduce_fusion.68
  288.5 4.1 dynamic-slice_reduce_fusion.69
  308.5 5.5 dynamic-slice_reduce_fusion.68
  319.9 4.1 dynamic-slice_reduce_fusion.69
  339.9 5.5 dynamic-slice_reduce_fusion.68
  351.4 4.1 dynamic-slice_reduce_fusion.69
  371.3 5.5 dynamic-slice_reduce_fusion.68
  382.8 4.1 dynamic-slice_reduce_fusion.69
  402.7 5.5 dynamic-slice_reduce_fusion.68
  414.2 4.1 dynamic-slice_reduce_fusion.69
  434.1 5.5 dynamic-slice_reduce_fusion.68
  445.6 4.1 dynamic-slice_reduce_fusion.69
  466.8 40.5 %while.69 = (s32[]{:T(128)}, f32[8,160,160]{2,1,0:T(8,128)}, bf16[8,128,128]{2,1,0:T(8,128)(2,1)}, bf16[8,5120,128]{2,1,0:T(8,128)(2,1)}, s32[]{:T(128)}) while((s32[]{:T(128)}, f32[8,160,160]{2,1,0:T(8,128)}, bf16[8,128,128]{2,1,0:T(8,128)(2,1)}, bf16[8,5120,128]{2,1,0:T(8,128)(2,1)}, s32[]{:T(128)}) %tuple.322), condition=%wide.region_12.13_spmd, body=%wide.region_11.12_spmd.sunk | while | flops 168565760 | bytes 15025217 | solution.py:161
  512.3 42.6 %all_to_all.34 = f32[8,2,25600]{2,1,0:T(2,128)S(1)} all-to-all(f32[8,2,25600]{2,1,0:T(2,128)S(1)} %copy.129), channel_id=1, replica_groups=mesh['ty'=4,'tx'=8] {'tx'}, dimensions={0} | all-to-all | bytes 3276800 | tf_op jit(solution)/shard_map/all_to_all | solution.py:163
  557.2 3.7 dot_general.74
  560.9 7.5 fusion.54
  595.8 11.4 collective-permute-done.10
  609.3 42.1 %all-reduce.127 = (f32[]{:T(128)}, f32[]{:T(128)}, f32[]{:T(128)}) all-reduce(f32[]{:T(128)} %get-tuple-element.314, f32[]{:T(128)} %get-tuple-element.313, f32[]{:T(128)} %get-tuple-element.312), channel_id=1, replica_groups=mesh['ty'=4,'tx'=8] {'ty','tx'}, use_global_device_ids=true, to_apply=%region_8.9 | all-reduce | flops 3 | bytes 24 | tf_op jit(solution)/shard_map/psum | solution.py:173
  658.7 4.3 collective-permute-done.13
  668.0 4.6 collective-permute-done.15
  682.0 5.5 all-to-all-start.4
  687.5 21.3 %all-to-all-done.4 = bf16[8,2,25600]{2,1,0:T(2,128)(2,1)S(1)} async-done(((bf16[8,2,25600]{2,1,0:T(2,128)(2,1)}), bf16[8,2,25600]{2,1,0:T(2,128)(2,1)S(1)}, u32[]{:S(2)}, u32[]{:S(2)}) %all-to-all-start.4) | async-done | bytes 819232 | tf_op jit(solution)/shard_map/all_to_all | solution.py:187
  710.2 251.3 %while.70 = (s32[]{:T(128)}, bf16[8,128,128]{2,1,0:T(8,128)(2,1)}, bf16[8,25600]{1,0:T(8,128)(2,1)S(1)}, bf16[8,5120,128]{2,1,0:T(8,128)(2,1)}, s32[]{:T(128)}, ...) while((s32[]{:T(128)}, bf16[8,128,128]{2,1,0:T(8,128)(2,1)}, ...), condition=%wide.region_18.19_spmd, body=%wide.region_17.18_spmd.sunk | while | flops 167772192 | bytes 10553141 | solution.py:193
  710.3 5.5 dynamic-slice_reduce_fusion.70
  721.9 4.1 dynamic-slice_reduce_fusion.71
  741.7 5.5 dynamic-slice_reduce_fusion.70
  753.2 4.1 dynamic-slice_reduce_fusion.71
  773.1 5.5 dynamic-slice_reduce_fusion.70
  784.6 4.1 dynamic-slice_reduce_fusion.71
  804.5 5.5 dynamic-slice_reduce_fusion.70
  816.0 4.1 dynamic-slice_reduce_fusion.71
  835.8 5.5 dynamic-slice_reduce_fusion.70
  847.3 4.1 dynamic-slice_reduce_fusion.71
  867.2 5.5 dynamic-slice_reduce_fusion.70
  878.7 4.1 dynamic-slice_reduce_fusion.71
  898.6 5.5 dynamic-slice_reduce_fusion.70
  910.1 4.1 dynamic-slice_reduce_fusion.71
  930.0 5.5 dynamic-slice_reduce_fusion.70
  941.4 4.1 dynamic-slice_reduce_fusion.71
  962.7 40.5 %while.71 = (s32[]{:T(128)}, f32[8,160,160]{2,1,0:T(8,128)}, bf16[8,128,128]{2,1,0:T(8,128)(2,1)}, bf16[8,5120,128]{2,1,0:T(8,128)(2,1)}, s32[]{:T(128)}) while((s32[]{:T(128)}, f32[8,160,160]{2,1,0:T(8,128)}, bf16[8,128,128]{2,1,0:T(8,128)(2,1)}, bf16[8,5120,128]{2,1,0:T(8,128)(2,1)}, s32[]{:T(128)}) %tuple.324), condition=%wide.region_20.21_spmd, body=%wide.region_19.20_spmd.sunk | while | flops 168565760 | bytes 15025217 | solution.py:161
  1008.2 42.6 %all_to_all.35 = f32[8,2,25600]{2,1,0:T(2,128)S(1)} all-to-all(f32[8,2,25600]{2,1,0:T(2,128)S(1)} %copy.139), channel_id=1, replica_groups=mesh['ty'=4,'tx'=8] {'tx'}, dimensions={0} | all-to-all | bytes 3276800 | tf_op jit(solution)/shard_map/all_to_all | solution.py:163
  1053.1 3.7 dot_general.80
  1056.8 7.6 fusion.57
  1091.6 11.4 collective-permute-done.18
  1106.0 42.0 %psum.34 = f32[]{:T(128)} all-reduce(f32[]{:T(128)} %multiply_reduce_fusion), channel_id=1, replica_groups=mesh['ty'=4,'tx'=8] {'ty','tx'}, use_global_device_ids=true, to_apply=%region_22.23 | all-reduce | flops 1 | bytes 8 | tf_op jit(solution)/shard_map/psum | solution.py:195
  (960 shorter events, 624.2 us)
Async XLA Ops:
  2.2 210.5 %copy-start.15 = (s32[8]{0:T(128)}, s32[8]{0:T(128)S(1)}, u32[]{:S(2)}) copy-start(s32[8]{0:T(128)S(1)} %get-tuple-element.491) | copy-start | bytes 100
  3.0 64.0 %all-to-all-start = ((s32[8,1,2]{2,1,0:T(1,128)}), s32[8,1,2]{2,1,0:T(1,128)S(1)}, u32[]{:S(2)}, u32[]{:S(2)}) async-start(s32[8,1,2]{2,1,0:T(1,128)} %bitcast.113), calls=%async_computation | async-start | bytes 8192 | tf_op jit(solution)/shard_map/all_to_all | solution.py:133
  11.8 51.2 %copy-start.21 = (s32[8,2]{0,1:T(2,128)}, s32[8,2]{0,1:T(2,128)S(1)}, u32[]{:S(2)}) copy-start(s32[8,2]{0,1:T(2,128)S(1)} %multiply_add_fusion.4) | copy-start | bytes 196
  14.1 18.6 %copy-start.8 = (f32[8,128,128]{2,1,0:T(8,128)S(1)}, f32[8,128,128]{2,1,0:T(8,128)}, u32[]{:S(2)}) copy-start(f32[8,128,128]{2,1,0:T(8,128)} %param.17) | copy-start | bytes 1572868
  67.0 44.1 %all-to-all-start.1 = ((f32[8,2,25600]{2,1,0:T(2,128)}), f32[8,2,25600]{2,1,0:T(2,128)S(1)}, u32[]{:S(2)}, u32[]{:S(2)}) async-start(f32[8,2,25600]{2,1,0:T(2,128)} %copy.119), calls=%async_computation.1 | async-start | bytes 3276800 | tf_op jit(solution)/shard_map/all_to_all | solution.py:163
  73.3 42.7 %copy-start.9 = (s32[4,4]{1,0:T(4,128)}, s32[4,4]{1,0:T(4,128)S(1)}, u32[]{:S(2)}) copy-start(s32[4,4]{1,0:T(4,128)S(1)} %multiply_add_fusion.3) | copy-start | bytes 196
  73.4 109.9 %copy-start.18 = (s32[16]{0:T(128)}, s32[16]{0:T(128)S(1)}, u32[]{:S(2)}) copy-start(s32[16]{0:T(128)S(1)} %sub.51) | copy-start | bytes 196
  124.9 1.2 copy-start.2
  127.2 1.8 slice-start
  133.7 1.2 copy-start.7
  135.1 2.6 collective-permute-start
  136.4 4.8 collective-permute-start.1
  141.4 15.3 %collective-permute-start.2 = (f32[576,16]{1,0:T(8,128)S(1)}, f32[576,16]{1,0:T(8,128)S(1)}, u32[]{:S(2)}, u32[]{:S(2)}) collective-permute-start(f32[576,16]{1,0:T(8,128)S(1)} %get-tuple-element.471), channel_id=1, source_target_pairs={{0,1},{1,2},{2,3},{3,4},{4,5},{5,6},{6,7},{8,9},{9,10},{10,11},{11... | collective-permute-start | bytes 110600 | tf_op jit(solution)/shard_map/ppermute | solution.py:21
  144.7 12.5 %copy-start.12 = (pred[512]{0:T(512)(128)(4,1)S(1)}, pred[512]{0:T(512)(128)(4,1)}, u32[]{:S(2)}) copy-start(pred[512]{0:T(512)(128)(4,1)} %constant.131.clone.1) | copy-start | bytes 1540
  144.8 11.9 %collective-permute-start.3 = (f32[576,16]{1,0:T(8,128)S(1)}, f32[576,16]{1,0:T(8,128)S(1)}, u32[]{:S(2)}, u32[]{:S(2)}) collective-permute-start(f32[576,16]{1,0:T(8,128)S(1)} %get-tuple-element.472), channel_id=1, source_target_pairs={{1,0},{2,1},{3,2},{4,3},{5,4},{6,5},{7,6},{9,8},{10,9},{11,10},{12... | collective-permute-start | bytes 110600 | tf_op jit(solution)/shard_map/ppermute | solution.py:22
  158.0 5.1 collective-permute-start.4
  161.8 3.1 collective-permute-start.5
  164.9 7.1 collective-permute-start.6
  169.1 7.7 collective-permute-start.7
  177.4 0.9 copy-start.5
  178.4 1.1 slice-start.3
  186.1 26.3 %all-to-all-start.2 = ((bf16[8,2,25600]{2,1,0:T(2,128)(2,1)}), bf16[8,2,25600]{2,1,0:T(2,128)(2,1)S(1)}, u32[]{:S(2)}, u32[]{:S(2)}) async-start(bf16[8,2,25600]{2,1,0:T(2,128)(2,1)} %reshape.371), calls=%async_computation.2 | async-start | bytes 1638400 | tf_op jit(solution)/shard_map/all_to_all | solution.py:187
  507.3 2.2 copy-start.16
  507.3 2.2 copy-start.22
  557.2 3.7 copy-start.10
  557.2 3.7 copy-start.19
  571.4 1.2 copy-start.3
  573.7 3.0 slice-start.1
  587.2 2.6 collective-permute-start.8
  588.5 3.1 collective-permute-start.9
  591.7 15.5 %collective-permute-start.10 = (f32[576,16]{1,0:T(8,128)S(1)}, f32[576,16]{1,0:T(8,128)S(1)}, u32[]{:S(2)}, u32[]{:S(2)}) collective-permute-start(f32[576,16]{1,0:T(8,128)S(1)} %get-tuple-element.469), channel_id=1, source_target_pairs={{0,1},{1,2},{2,3},{3,4},{4,5},{5,6},{6,7},{8,9},{9,10},{10,11},{11... | collective-permute-start | bytes 110600 | tf_op jit(solution)/shard_map/ppermute | solution.py:21
  594.5 13.2 %copy-start.13 = (pred[512]{0:T(512)(128)(4,1)S(1)}, pred[512]{0:T(512)(128)(4,1)}, u32[]{:S(2)}) copy-start(pred[512]{0:T(512)(128)(4,1)} %constant.131.clone.1) | copy-start | bytes 1540
  594.5 12.7 %collective-permute-start.11 = (f32[576,16]{1,0:T(8,128)S(1)}, f32[576,16]{1,0:T(8,128)S(1)}, u32[]{:S(2)}, u32[]{:S(2)}) collective-permute-start(f32[576,16]{1,0:T(8,128)S(1)} %get-tuple-element.470), channel_id=1, source_target_pairs={{1,0},{2,1},{3,2},{4,3},{5,4},{6,5},{7,6},{9,8},{10,9},{11,10},{12... | collective-permute-start | bytes 110600 | tf_op jit(solution)/shard_map/ppermute | solution.py:22
  609.3 63.9 %copy-start = (f32[512,512]{1,0:T(8,128)}, f32[512,512]{1,0:T(8,128)S(1)}, u32[]{:S(2)}) copy-start(f32[512,512]{1,0:T(8,128)S(1)} %get-tuple-element.366) | copy-start | bytes 3145732
  655.7 3.0 collective-permute-start.12
  657.4 5.6 collective-permute-start.13
  663.0 4.9 collective-permute-start.14
  665.4 7.2 collective-permute-start.15
  673.3 0.9 copy-start.6
  674.2 1.1 slice-start.4
  682.0 26.8 %all-to-all-start.4 = ((bf16[8,2,25600]{2,1,0:T(2,128)(2,1)}), bf16[8,2,25600]{2,1,0:T(2,128)(2,1)S(1)}, u32[]{:S(2)}, u32[]{:S(2)}) async-start(bf16[8,2,25600]{2,1,0:T(2,128)(2,1)} %reshape.385), calls=%async_computation.4 | async-start | bytes 1638400 | tf_op jit(solution)/shard_map/all_to_all | solution.py:187
  1003.2 2.2 copy-start.17
  1003.2 2.2 copy-start.23
  1053.1 3.7 copy-start.11
  1053.1 3.7 copy-start.20
  1067.4 1.2 copy-start.4
  1069.7 2.9 slice-start.2
  1083.0 2.6 collective-permute-start.16
  1084.3 3.1 collective-permute-start.17
  1087.6 15.5 %collective-permute-start.18 = (f32[576,16]{1,0:T(8,128)S(1)}, f32[576,16]{1,0:T(8,128)S(1)}, u32[]{:S(2)}, u32[]{:S(2)}) collective-permute-start(f32[576,16]{1,0:T(8,128)S(1)} %get-tuple-element.467), channel_id=1, source_target_pairs={{0,1},{1,2},{2,3},{3,4},{4,5},{5,6},{6,7},{8,9},{9,10},{10,11},{11... | collective-permute-start | bytes 110600 | tf_op jit(solution)/shard_map/ppermute | solution.py:21
  1090.3 13.3 %copy-start.14 = (pred[512]{0:T(512)(128)(4,1)S(1)}, pred[512]{0:T(512)(128)(4,1)}, u32[]{:S(2)}) copy-start(pred[512]{0:T(512)(128)(4,1)} %constant.131.clone.1) | copy-start | bytes 1540
  1090.3 12.7 %collective-permute-start.19 = (f32[576,16]{1,0:T(8,128)S(1)}, f32[576,16]{1,0:T(8,128)S(1)}, u32[]{:S(2)}, u32[]{:S(2)}) collective-permute-start(f32[576,16]{1,0:T(8,128)S(1)} %get-tuple-element.468), channel_id=1, source_target_pairs={{1,0},{2,1},{3,2},{4,3},{5,4},{6,5},{7,6},{9,8},{10,9},{11,10},{12... | collective-permute-start | bytes 110600 | tf_op jit(solution)/shard_map/ppermute | solution.py:22
  1103.6 1.2 copy-start.1
where the time goes:
time: 1170 us; the launch traced here: 1150 us
  local copies, waits for them, and re-layouts  617 us (53%)
  blocking collectives  169 us (14%)
  waiting for transfers between devices  139 us (12%)
  matrix products  96.1 us (8%)
  starting transfers between devices  61.6 us (5%)
  other arithmetic  59.2 us (5%)
    slice x544, local copies, waits for them, and re-layouts, forward_block(): framed[offset:offset + block_side]  416 us
    all_to_all x2, blocking collectives, adjoint_pass(): lax.all_to_all(outgoing.reshape(tx_size, capacity, -1), 'tx', split_axis=...  85.2 us
    concatenate x16, local copies, waits for them, and re-layouts, forward_block(): jnp.concatenate([framed[offset:offset + block_side] for offset in range(t...  46.5 us
    all_to_all x2, waiting for transfers between devices, body(): lax.all_to_all(pieces, 'tx', split_axis=0, concat_axis=0, tiled=True)  42.7 us
    psum x1, blocking collectives, body(): norm_now = lax.psum(jnp.sum(residual * residual), ('ty', 'tx'))  42.1 us
    psum x1, blocking collectives, body(): lax.psum((jnp.sum(direction * applied), jnp.sum(residual * applied), jnp....  42 us
    dot_general x16, matrix products, forward_block(): return jnp.dot(stacked, banded, preferred_element_type=jnp.float32)  38.9 us
    all_to_all x1, waiting for transfers between devices, adjoint_pass(): lax.all_to_all(outgoing.reshape(tx_size, capacity, -1), 'tx', split_axis=...  37.7 us
  transfers between devices with their start and end apart: 24, of which 15 were waited for; matrix products, arithmetic and copies ran while one was open for 5% of the time, Pallas kernels for 0%

commit v1 on v0

v1 whole, which is shorter than its diff:
```python
import functools

import jax
import jax.numpy as jnp
from jax import lax
from jax.experimental import pallas as pl
from jax.experimental.pallas import tpu as pltpu
from jax.sharding import PartitionSpec as P

TILE = 512
SUB = 4
ITERS = 2
GROUP = 32
LANES = 128

damping = 0.05


def make_kernels(point_spread, warp_steps):
    tap_count = point_spread.shape[-1] + 1
    totals = jnp.sum(point_spread, axis=(1, 2), keepdims=True)
    padded = jnp.pad(point_spread / totals, ((0, 0), (0, 1), (0, 1)))
    row_frac = (warp_steps[:, 0].astype(jnp.float32) / SUB)[:, None, None]
    col_frac = (warp_steps[:, 1].astype(jnp.float32) / SUB)[:, None, None]
    shifted = jnp.pad(padded, ((0, 0), (0, 0), (1, 0)))[:, :, :tap_count]
    blended = (1.0 - col_frac) * padded + col_frac * shifted
    lowered = jnp.pad(blended, ((0, 0), (1, 0), (0, 0)))[:, :tap_count, :]
    return ((1.0 - row_frac) * blended + row_frac * lowered).astype(jnp.bfloat16)


def turn(value, shift, axis):
    size = value.shape[axis]
    shift = shift % size
    return value if shift == 0 else pltpu.roll(value, shift, axis)


def lane_group(shape, width):
    return lax.broadcasted_iota(jnp.int32, shape, 1) // width


def pick_groups(groups, parts):
    value = parts[-1]
    for number in range(len(parts) - 2, -1, -1):
        value = jnp.where(groups == number, parts[number], value)
    return value


def toeplitz(rows):
    tiles = []
    for j in range(8):
        halves = []
        for half in range(2):
            spread = jnp.broadcast_to(rows[2 * j + half : 2 * j + half + 1], (GROUP, LANES))
            halves.append(pltpu.roll(spread, 0, 1, stride=1, stride_axis=0))
        tiles.append(jnp.concatenate(halves, axis=1))
    return jnp.concatenate(tiles, axis=0).astype(jnp.bfloat16)


def blur(left, right, matrix):
    groups = lane_group(left.shape, GROUP)
    low = groups < 2
    by32, by64, by96 = turn(left, 32, 1), turn(left, 64, 1), turn(left, 96, 1)
    end32, end96 = turn(right, 32, 1), turn(right, 96, 1)
    framed = [
        jnp.where(low, left, by64),
        jnp.where(low, by96, by32),
        jnp.where(low, by64, left),
        pick_groups(groups, [by32, end32, by96, end96]),
    ]
    summed = []
    for part in framed:
        first = jnp.where(low, part, turn(part, -1, 0))
        stacked = jnp.concatenate([first, turn(first, -2, 0)], axis=1).astype(jnp.bfloat16)
        product = lax.dot_general(
            stacked, matrix, (((1,), (1,)), ((), ())), preferred_element_type=jnp.float32
        )
        joined = product[:, :LANES] + turn(product[:, LANES:], -16, 0)
        summed.append(pick_groups(groups, [turn(joined, -4 * j, 0) for j in range(4)]))
    total = pick_groups(groups, summed)
    for step in range(1, 4):
        chosen = pick_groups(groups, [summed[(j + step) % 4] for j in range(4)])
        total = total + turn(chosen, 32 * step, 1)
    return total


def blur_back(image, matrix):
    groups = lane_group(image.shape, GROUP)
    low = groups < 2
    turned = [turn(image, 32 * step, 1) for step in range(4)]
    folded = []
    for h in range(4):
        spread = pick_groups(groups, [turned[(j - h) % 4] for j in range(4)])
        first = pick_groups(groups, [turn(spread, 4 * j, 0) for j in range(4)])
        stacked = jnp.concatenate([first, turn(first, 16, 0)], axis=1).astype(jnp.bfloat16)
        product = jnp.dot(stacked, matrix, preferred_element_type=jnp.float32)
        joined = product[:, :LANES] + turn(product[:, LANES:], 2, 0)
        shifted = jnp.where(low, joined, turn(joined, 1, 0))
        folded.append(shifted + turn(shifted, 64, 1))
    one, three = turn(folded[1], 32, 1), turn(folded[3], 32, 1)
    zero = jnp.zeros_like(one)
    left = jnp.where(low, folded[0], folded[2]) + pick_groups(groups, [zero, one, one, three])
    right = jnp.where(groups == 0, three, 0.0)
    return left, right


def place(total_ref, cell, per_row, block, patch):
    left, right = patch
    rows = pl.ds(pl.multiple_of(cell // per_row * block, block), left.shape[0])
    start = pl.multiple_of(cell % per_row * block, block)
    total_ref[rows, pl.ds(start, block)] += left
    total_ref[rows, pl.ds(pl.multiple_of(start + block, block), block)] += right


def pack_kernel(count, source_ref, tag_ref, exposures_ref, taps_ref, out_ref):
    block = exposures_ref.shape[1]

    @pl.loop(0, count)
    def _(slot):
        origin = source_ref[slot]
        out_ref[slot, :block, :] = exposures_ref[origin].astype(jnp.bfloat16)
        out_ref[slot, block : block + 16, :] = taps_ref[origin]
        out_ref[slot, block + 16 :, :] = jnp.full((16, LANES), tag_ref[slot], jnp.float32).astype(
            jnp.bfloat16
        )


def first_kernel(count, per_row, block, cell_ref, frames_ref, total_ref, matrix_ref):
    total_ref[...] = jnp.zeros_like(total_ref)

    @pl.loop(0, count)
    def _(slot):
        cell = cell_ref[slot]

        @pl.when(cell >= 0)
        def _():
            frame = frames_ref[slot]
            matrix = toeplitz(frame[block : block + 16].astype(jnp.float32))
            matrix_ref[slot] = matrix
            image = frame[:block].astype(jnp.float32)
            image = jnp.concatenate([image, jnp.zeros((GROUP, LANES), jnp.float32)], axis=0)
            place(total_ref, cell, per_row, block, blur_back(image, matrix))


def normal_kernel(count, per_row, block, cell_ref, field_ref, matrix_ref, total_ref):
    total_ref[...] = jnp.zeros_like(total_ref)
    window = block + GROUP

    @pl.loop(0, count)
    def _(slot):
        cell = cell_ref[slot]

        @pl.when(cell >= 0)
        def _():
            matrix = matrix_ref[slot]
            rows = pl.ds(pl.multiple_of(cell // per_row * block, block), window)
            start = pl.multiple_of(cell % per_row * block, block)
            left = field_ref[rows, pl.ds(start, block)].astype(jnp.float32)
            right = field_ref[rows, pl.ds(pl.multiple_of(start + block, block), block)].astype(
                jnp.float32
            )
            modelled = blur(left, right, matrix).astype(jnp.bfloat16).astype(jnp.float32)
            inside = lax.broadcasted_iota(jnp.int32, modelled.shape, 0) < block
            image = jnp.where(inside, modelled, 0.0)
            place(total_ref, cell, per_row, block, blur_back(image, matrix))


def vmem():
    return pl.BlockSpec(memory_space=pltpu.VMEM)


def smem():
    return pl.BlockSpec(memory_space=pltpu.SMEM)


def share_edges(value, axis, dim, width):
    size, length = lax.axis_size(axis), value.shape[dim]
    position = lax.axis_index(axis)
    up = [(i, i + 1) for i in range(size - 1)]
    down = [(j, i) for i, j in up]
    first = lax.slice_in_dim(value, 0, 2 * width, axis=dim)
    middle = lax.slice_in_dim(value, 2 * width, length - 2 * width, axis=dim)
    last = lax.slice_in_dim(value, length - 2 * width, length, axis=dim)
    before = lax.ppermute(last, axis, up)
    after = lax.ppermute(first, axis, down)
    index = lax.broadcasted_iota(jnp.int32, first.shape, dim)
    first = jnp.where((position > 0) | (index >= width), first + before, 0.0)
    last = jnp.where((position < size - 1) | (index < width), last + after, 0.0)
    return jnp.concatenate([first, middle, last], axis=dim)


def body(exposures, point_spread, warp_steps, column, block_cell):
    frame_count, block = exposures.shape[:2]
    tap_count = point_spread.shape[1] + 1
    margin = tap_count // 2
    tx_size = lax.axis_size("tx")
    capacity = max(2, 2 * frame_count // tx_size)
    slot_count = tx_size * capacity
    per_row = TILE // block
    extent = TILE + 2 * margin
    wide = TILE + block
    taps = make_kernels(point_spread, warp_steps)
    taps = jnp.pad(taps, ((0, 0), (0, 0), (0, 64 - tap_count))).reshape(frame_count, 16, LANES)

    target = column[:, 0]
    earlier = jnp.arange(frame_count)[:, None] > jnp.arange(frame_count)[None, :]
    matching = target[:, None] == target[None, :]
    standing = jnp.sum(jnp.where(earlier & matching, 1, 0), axis=1)
    slot_index = target * capacity + standing
    chosen = slot_index[None, :] == jnp.arange(slot_count)[:, None]
    source = jnp.sum(jnp.where(chosen, jnp.arange(frame_count)[None, :], 0), axis=1).astype(jnp.int32)
    tag = jnp.sum(jnp.where(chosen, block_cell[None, :] + 1, 0), axis=1).astype(jnp.float32)

    packed = pl.pallas_call(
        functools.partial(pack_kernel, slot_count),
        out_shape=jax.ShapeDtypeStruct((slot_count, block + 32, LANES), jnp.bfloat16),
        in_specs=[smem(), smem(), vmem(), vmem()],
        out_specs=vmem(),
        name="pack",
    )(source, tag, exposures, taps)
    frames = lax.all_to_all(packed, "tx", split_axis=0, concat_axis=0, tiled=True)
    cells = frames[:, block + 16, 0].astype(jnp.int32) - 1

    total, matrices = pl.pallas_call(
        functools.partial(first_kernel, slot_count, per_row, block),
        out_shape=(
            jax.ShapeDtypeStruct((extent, wide), jnp.float32),
            jax.ShapeDtypeStruct((slot_count, 256, 256), jnp.bfloat16),
        ),
        in_specs=[smem(), vmem()],
        out_specs=(vmem(), vmem()),
        name="first_adjoint",
    )(cells, frames)

    def finish(total):
        value = share_edges(total[:, :extent], "ty", 0, margin)
        return share_edges(value, "tx", 1, margin)

    def inner(value):
        return value[margin : margin + TILE, margin : margin + TILE]

    def products(pairs):
        return tuple(jnp.sum(inner(left * right)) for left, right in pairs)

    residual = finish(total)
    direction = residual
    solution = jnp.zeros((TILE, TILE), jnp.float32)
    norm_now = None
    for iteration in range(ITERS):
        field = jnp.pad(direction.astype(jnp.bfloat16), ((0, 0), (0, wide - extent)))
        total = pl.pallas_call(
            functools.partial(normal_kernel, slot_count, per_row, block),
            out_shape=jax.ShapeDtypeStruct((extent, wide), jnp.float32),
            in_specs=[smem(), vmem(), vmem()],
            out_specs=vmem(),
            name="normal",
        )(cells, field, matrices)
        applied = finish(total) + damping * direction
        last = iteration + 1 == ITERS
        pairs = [(direction, applied)]
        if not last:
            pairs = pairs + [(residual, applied), (applied, applied)]
        if norm_now is None:
            pairs = pairs + [(residual, residual)]
        sums = lax.psum(jnp.stack(products(pairs)), ("ty", "tx"))
        if norm_now is None:
            norm_now = sums[-1]
        step_size = norm_now / sums[0]
        solution = solution + step_size * inner(direction)
        residual = residual - step_size * applied
        if not last:
            norm_next = norm_now - 2.0 * step_size * sums[1] + step_size * step_size * sums[2]
            direction = residual + norm_next / norm_now * direction
            norm_now = norm_next
    return solution, inner(residual)


def solution(mesh):
    placed = (
        P(("ty", "tx"), None, None),
        P(("ty", "tx"), None, None),
        P(("ty", "tx"), None),
        P(("ty", "tx"), None),
        P(("ty", "tx")),
    )
    return jax.shard_map(
        body, mesh=mesh, in_specs=placed, out_specs=(P("ty", "tx"), P("ty", "tx")), check_vma=False
    )
```

time: 1170 us -> 266 us (0.23); the launches traced: 1150 us -> 264 us
  local copies, waits for them, and re-layouts: 617 us -> 12.9 us
  matrix products: 96.1 us -> 0 us
  blocking collectives: 169 us -> 78.1 us
  waiting for transfers between devices: 139 us -> 65.3 us
  other arithmetic: 59.2 us -> 21.7 us
  Pallas kernels: 0 us -> 25 us
    slice x583 -> x7, local copies, waits for them, and re-layouts: 419 us -> 7.57 us  [the longest x3 4.11 us: share_edges(): middle = lax.slice_in_dim(value, 2 * width, length - 2 * width, axis=dim)]
    dot_general x58 -> x0, matrix products: 96.1 us -> none  [the longest x16 38.9 us: forward_block(): return jnp.dot(stacked, banded, preferred_element_type=jnp.float32)]
    all_to_all x2 -> x0, blocking collectives: 85.2 us -> none  [adjoint_pass(): lax.all_to_all(outgoing.reshape(tx_size, capacity, -1), 'tx', split_axis=...]
    all_to_all x4 -> x1, waiting for transfers between devices: 80.3 us -> 17.3 us  [body(): lax.all_to_all(packed, 'tx', split_axis=0, concat_axis=0, tiled=True)]
    reshape x27 -> x1, local copies, waits for them, and re-layouts: 51.6 us -> 0.71 us  [body(): jnp.pad(taps, ((0, 0), (0, 0), (0, 64 - tap_count)))]
    concatenate x20 -> x0, local copies, waits for them, and re-layouts: 47.6 us -> none  [the longest x16 46.5 us: forward_block(): jnp.concatenate([framed[offset:offset + block_side] for offset in range(t...]
    dynamic_slice x24 -> x0, local copies, waits for them, and re-layouts: 33.7 us -> none  [adjoint_pass(): lax.map(apply_back, (images_low, frame_bands)).reshape(frame_count, -1)]
    broadcast_in_dim x25 -> x0, other arithmetic: 33.5 us -> none  [the longest x24 33.5 us: adjoint_pass(): lax.map(apply_back, (images_low, frame_bands)).reshape(frame_count, -1)]
  transfers between devices with their start and end apart: 24 -> 13, of which waited for: 15 -> 10; matrix products, arithmetic and copies ran while one was open for 5% -> 2% of each run, Pallas kernels for 0% -> 0%
where the time goes in v1:
time: 266 us; the launch traced here: 264 us
  blocking collectives  78.1 us (29%)
  waiting for transfers between devices  65.3 us (25%)
  starting transfers between devices  55.5 us (21%)
  Pallas kernels  25 us (9%)
  other arithmetic  21.7 us (8%)
  local copies, waits for them, and re-layouts  12.9 us (5%)
  between operations  5.47 us (2%)
    psum x2, blocking collectives, body(): sums = lax.psum(jnp.stack(products(pairs)), ('ty', 'tx'))  78.1 us
    ppermute x6, starting transfers between devices, share_edges(): before = lax.ppermute(last, axis, up)  40.5 us
    ppermute x6, waiting for transfers between devices, share_edges(): after = lax.ppermute(first, axis, down)  32.8 us
    all_to_all x1, waiting for transfers between devices, body(): lax.all_to_all(packed, 'tx', split_axis=0, concat_axis=0, tiled=True)  17.3 us
    pallas_call x2, Pallas kernels, body(): pl.pallas_call(functools.partial(normal_kernel, slot_count, per_row, bloc...  16.8 us
    ppermute x6, waiting for transfers between devices, share_edges(): before = lax.ppermute(last, axis, up)  15.2 us
    ppermute x6, starting transfers between devices, share_edges(): after = lax.ppermute(first, axis, down)  7.75 us
    all_to_all x1, starting transfers between devices, body(): lax.all_to_all(packed, 'tx', split_axis=0, concat_axis=0, tiled=True)  7.31 us
  transfers between devices with their start and end apart: 13, of which 10 were waited for; matrix products, arithmetic and copies ran while one was open for 2% of the time, Pallas kernels for 0%

profile of v1, /device:TPU:0, one launch (start us, length us, event | category | flops | bytes accessed | tf_op | source)
XLA Modules:
  0.0 263.9 jit_solution(12608812840584460578)
XLA Ops:
  0.6 0.8 broadcast_subtract_fusion.1
  1.4 0.8 multiply_bitcast_fusion.1
  2.2 0.9 select_reduce_fusion.2
  3.1 0.7 multiply_add_fusion.3
  3.7 0.6 select_reduce_fusion
  4.3 0.6 convert_element_type.49.tag_ref
  4.9 1.1 reduce_sum.79
  6.0 1.0 broadcast_divide_fusion
  7.0 0.1 multiply_add_fusion.2
  7.2 0.7 reshape.50.taps_ref
  8.0 2.0 pack.1
  10.0 7.3 %all-to-all-start = ((bf16[16,160,128]{2,1,0:T(8,128)(2,1)}), bf16[16,160,128]{2,1,0:T(8,128)(2,1)S(1)}, u32[]{:S(2)}, u32[]{:S(2)}) async-start(bf16[16,160,128]{2,1,0:T(8,128)(2,1)} %pack.1), calls=%async_computation | async-start | bytes 1310720 | tf_op jit(solution)/shard_map/all_to_all | solution.py:220
  17.3 17.3 %all-to-all-done.frames_ref = bf16[16,160,128]{2,1,0:T(8,128)(2,1)S(1)} async-done(((bf16[16,160,128]{2,1,0:T(8,128)(2,1)}), bf16[16,160,128]{2,1,0:T(8,128)(2,1)S(1)}, u32[]{:S(2)}, u32[]{:S(2)}) %all-to-all-start) | async-done | bytes 655392 | tf_op jit(solution)/shard_map/all_to_all | solution.py:220
  34.6 0.9 fusion.13.cell_ref
  35.5 6.2 %first_adjoint.1 = (f32[544,640]{1,0:T(8,128)}, bf16[16,256,256]{2,1,0:T(8,128)(2,1)}) custom-call(s32[16]{0:T(128)} %fusion.13.cell_ref, bf16[16,160,128]{2,1,0:T(8,128)(2,1)} %copy-done.4), custom_call_target="tpu_custom_call" | custom-call | tf_op jit(solution)/shard_map/first_adjoint/pallas_call | solution.py:223
  41.7 0.9 fusion.20
  42.6 1.3 collective-permute-start
  43.9 1.3 collective-permute-start.1
  45.3 1.4 slice.122
  46.6 2.2 collective-permute-done.1
  48.8 1.0 add_select_fusion.11
  49.9 8.4 %collective-permute-start.2 = (f32[544,32]{1,0:T(8,128)S(1)}, f32[544,32]{1,0:T(8,128)S(1)}, u32[]{:S(2)}, u32[]{:S(2)}) collective-permute-start(f32[544,32]{1,0:T(8,128)S(1)} %pad_maximum_fusion.4), channel_id=1, source_target_pairs={{0,1},{1,2},{2,3},{3,4},{4,5},{5,6},{6,7},{8,9},{9,10},{10,11},{11... | collective-permute-start | bytes 208904 | tf_op jit(solution)/shard_map/ppermute | solution.py:183
  58.3 4.9 %collective-permute-done.2 = f32[544,32]{1,0:T(8,128)S(1)} collective-permute-done((f32[544,32]{1,0:T(8,128)S(1)}, f32[544,32]{1,0:T(8,128)S(1)}, u32[]{:S(2)}, u32[]{:S(2)}) %collective-permute-start.2) | collective-permute-done | bytes 69664 | tf_op jit(solution)/shard_map/ppermute | solution.py:183
  63.2 1.3 collective-permute-start.3
  64.5 9.3 %collective-permute-done.3 = f32[544,32]{1,0:T(8,128)S(1)} collective-permute-done((f32[544,32]{1,0:T(8,128)S(1)}, f32[544,32]{1,0:T(8,128)S(1)}, u32[]{:S(2)}, u32[]{:S(2)}) %collective-permute-start.3) | collective-permute-done | bytes 69664 | tf_op jit(solution)/shard_map/ppermute | solution.py:184
  73.9 0.2 fusion.16
  74.1 0.9 pad.27.field_ref
  75.0 8.4 %normal.2 = f32[544,640]{1,0:T(8,128)} custom-call(s32[16]{0:T(128)} %fusion.13.cell_ref, bf16[544,640]{1,0:T(8,128)(2,1)} %pad.27.field_ref, bf16[16,256,256]{2,1,0:T(8,128)(2,1)} %get-tuple-element.5.matrix_ref), custom_call_target="tpu_custom_call" | custom-call | tf_op jit(solution)/shard_map/normal/pallas_call | solution.py:250
  83.4 0.9 fusion.19
  84.3 4.7 %collective-permute-start.4 = (f32[32,544]{1,0:T(8,128)S(1)}, f32[32,544]{1,0:T(8,128)S(1)}, u32[]{:S(2)}, u32[]{:S(2)}) collective-permute-start(f32[32,544]{1,0:T(8,128)S(1)} %get-tuple-element.28), channel_id=1, source_target_pairs={{0,8},{8,16},{16,24},{1,9},{9,17},{17,25},{2,10},{10,18},{18,26},{... | collective-permute-start | bytes 208904 | tf_op jit(solution)/shard_map/ppermute | solution.py:183
  89.0 1.3 collective-permute-start.5
  90.3 1.4 slice.152
  91.7 0.5 collective-permute-done.5
  92.2 1.0 add_select_fusion.9
  93.2 11.7 %collective-permute-start.6 = (f32[544,32]{1,0:T(8,128)S(1)}, f32[544,32]{1,0:T(8,128)S(1)}, u32[]{:S(2)}, u32[]{:S(2)}) collective-permute-start(f32[544,32]{1,0:T(8,128)S(1)} %pad_maximum_fusion.2), channel_id=1, source_target_pairs={{0,1},{1,2},{2,3},{3,4},{4,5},{5,6},{6,7},{8,9},{9,10},{10,11},{11... | collective-permute-start | bytes 208904 | tf_op jit(solution)/shard_map/ppermute | solution.py:183
  105.0 5.4 %collective-permute-done.6 = f32[544,32]{1,0:T(8,128)S(1)} collective-permute-done((f32[544,32]{1,0:T(8,128)S(1)}, f32[544,32]{1,0:T(8,128)S(1)}, u32[]{:S(2)}, u32[]{:S(2)}) %collective-permute-start.6) | collective-permute-done | bytes 69664 | tf_op jit(solution)/shard_map/ppermute | solution.py:183
  110.4 1.3 collective-permute-start.7
  111.7 9.8 %collective-permute-done.7 = f32[544,32]{1,0:T(8,128)S(1)} collective-permute-done((f32[544,32]{1,0:T(8,128)S(1)}, f32[544,32]{1,0:T(8,128)S(1)}, u32[]{:S(2)}, u32[]{:S(2)}) %collective-permute-start.7) | collective-permute-done | bytes 69664 | tf_op jit(solution)/shard_map/ppermute | solution.py:184
  121.6 0.2 fusion.5
  121.8 1.1 copy-done
  122.9 1.2 multiply_reduce_fusion.3
  124.2 2.0 pad_maximum_fusion.6
  126.1 38.9 %psum.14 = f32[4]{0:T(128)S(1)} all-reduce(f32[4]{0:T(128)S(1)} %pad_maximum_fusion.6), channel_id=1, replica_groups=mesh['ty'=4,'tx'=8] {'ty','tx'}, use_global_device_ids=true, to_apply=%region_7.8 | all-reduce | flops 4 | bytes 32 | tf_op jit(solution)/shard_map/psum | solution.py:264
  165.0 0.7 fusion.21
  169.5 2.7 %fusion.15 = (bf16[544,544]{1,0:T(8,128)(2,1)S(1)}, f32[544,544]{1,0:T(8,128)S(1)}, f32[544,544]{1,0:T(8,128)}) fusion(f32[544,544]{1,0:T(8,128)S(1)} %get-tuple-element.19, f32[]{:T(128)S(6)} %div.34, f32[544,544]{1,0:T(8,128)} %copy-done, f32[]{:T(128)S(6)} %div.33), kind=kLoop, calls=%fused_computation.69 | loop fusion | flops 1479680 | bytes 5326856 | tf_op jit(solution)/shard_map/convert_element_type | solution.py:249
  172.2 0.9 pad.28.field_ref
  173.1 8.4 %normal.3 = f32[544,640]{1,0:T(8,128)} custom-call(s32[16]{0:T(128)} %fusion.13.cell_ref, bf16[544,640]{1,0:T(8,128)(2,1)} %pad.28.field_ref, bf16[16,256,256]{2,1,0:T(8,128)(2,1)} %get-tuple-element.5.matrix_ref), custom_call_target="tpu_custom_call" | custom-call | tf_op jit(solution)/shard_map/normal/pallas_call | solution.py:250
  181.5 0.9 fusion.18
  182.5 2.6 %collective-permute-start.8 = (f32[32,544]{1,0:T(8,128)S(1)}, f32[32,544]{1,0:T(8,128)S(1)}, u32[]{:S(2)}, u32[]{:S(2)}) collective-permute-start(f32[32,544]{1,0:T(8,128)S(1)} %get-tuple-element.24), channel_id=1, source_target_pairs={{0,8},{8,16},{16,24},{1,9},{9,17},{17,25},{2,10},{10,18},{18,26},{... | collective-permute-start | bytes 208904 | tf_op jit(solution)/shard_map/ppermute | solution.py:183
  185.1 1.3 collective-permute-start.9
  186.4 1.4 slice.160
  187.8 1.6 collective-permute-done.9
  189.4 1.0 add_select_fusion.7
  190.5 11.6 %collective-permute-start.10 = (f32[544,32]{1,0:T(8,128)S(1)}, f32[544,32]{1,0:T(8,128)S(1)}, u32[]{:S(2)}, u32[]{:S(2)}) collective-permute-start(f32[544,32]{1,0:T(8,128)S(1)} %pad_maximum_fusion), channel_id=1, source_target_pairs={{0,1},{1,2},{2,3},{3,4},{4,5},{5,6},{6,7},{8,9},{9,10},{10,11},{11... | collective-permute-start | bytes 208904 | tf_op jit(solution)/shard_map/ppermute | solution.py:183
  202.1 4.9 %collective-permute-done.10 = f32[544,32]{1,0:T(8,128)S(1)} collective-permute-done((f32[544,32]{1,0:T(8,128)S(1)}, f32[544,32]{1,0:T(8,128)S(1)}, u32[]{:S(2)}, u32[]{:S(2)}) %collective-permute-start.10) | collective-permute-done | bytes 69664 | tf_op jit(solution)/shard_map/ppermute | solution.py:183
  207.1 1.3 collective-permute-start.11
  208.4 9.3 %collective-permute-done.11 = f32[544,32]{1,0:T(8,128)S(1)} collective-permute-done((f32[544,32]{1,0:T(8,128)S(1)}, f32[544,32]{1,0:T(8,128)S(1)}, u32[]{:S(2)}, u32[]{:S(2)}) %collective-permute-start.11) | collective-permute-done | bytes 69664 | tf_op jit(solution)/shard_map/ppermute | solution.py:184
  217.7 0.2 fusion.2
  218.0 1.1 copy-done.1
  219.1 1.2 multiply_reduce_fusion
  220.3 39.2 %psum.15 = f32[]{:T(128)} all-reduce(f32[]{:T(128)} %multiply_reduce_fusion), channel_id=1, replica_groups=mesh['ty'=4,'tx'=8] {'ty','tx'}, use_global_device_ids=true, to_apply=%region_9.10 | all-reduce | flops 1 | bytes 8 | tf_op jit(solution)/shard_map/psum | solution.py:264
  260.2 1.6 multiply_add_fusion.1
  261.8 0.5 copy-done.3
  262.3 1.6 slice_subtract_fusion
  (26 shorter events, 0.5 us)
Async XLA Ops:
  10.0 24.6 %all-to-all-start = ((bf16[16,160,128]{2,1,0:T(8,128)(2,1)}), bf16[16,160,128]{2,1,0:T(8,128)(2,1)S(1)}, u32[]{:S(2)}, u32[]{:S(2)}) async-start(bf16[16,160,128]{2,1,0:T(8,128)(2,1)} %pack.1), calls=%async_computation | async-start | bytes 1310720 | tf_op jit(solution)/shard_map/all_to_all | solution.py:220
  34.6 0.9 copy-start.4
  42.6 4.0 %collective-permute-start = (f32[32,544]{1,0:T(8,128)S(1)}, f32[32,544]{1,0:T(8,128)S(1)}, u32[]{:S(2)}, u32[]{:S(2)}) collective-permute-start(f32[32,544]{1,0:T(8,128)S(1)} %get-tuple-element.32), channel_id=1, source_target_pairs={{0,8},{8,16},{16,24},{1,9},{9,17},{17,25},{2,10},{10,18},{18,26},{... | collective-permute-start | bytes 208904 | tf_op jit(solution)/shard_map/ppermute | solution.py:183
  43.9 4.9 %collective-permute-start.1 = (f32[32,544]{1,0:T(8,128)S(1)}, f32[32,544]{1,0:T(8,128)S(1)}, u32[]{:S(2)}, u32[]{:S(2)}) collective-permute-start(f32[32,544]{1,0:T(8,128)S(1)} %get-tuple-element.33), channel_id=1, source_target_pairs={{8,0},{16,8},{24,16},{9,1},{17,9},{25,17},{10,2},{18,10},{26,18},{... | collective-permute-start | bytes 208904 | tf_op jit(solution)/shard_map/ppermute | solution.py:184
  49.9 13.3 %collective-permute-start.2 = (f32[544,32]{1,0:T(8,128)S(1)}, f32[544,32]{1,0:T(8,128)S(1)}, u32[]{:S(2)}, u32[]{:S(2)}) collective-permute-start(f32[544,32]{1,0:T(8,128)S(1)} %pad_maximum_fusion.4), channel_id=1, source_target_pairs={{0,1},{1,2},{2,3},{3,4},{4,5},{5,6},{6,7},{8,9},{9,10},{10,11},{11... | collective-permute-start | bytes 208904 | tf_op jit(solution)/shard_map/ppermute | solution.py:183
  63.2 10.6 %collective-permute-start.3 = (f32[544,32]{1,0:T(8,128)S(1)}, f32[544,32]{1,0:T(8,128)S(1)}, u32[]{:S(2)}, u32[]{:S(2)}) collective-permute-start(f32[544,32]{1,0:T(8,128)S(1)} %get-tuple-element.21), channel_id=1, source_target_pairs={{1,0},{2,1},{3,2},{4,3},{5,4},{6,5},{7,6},{9,8},{10,9},{11,10},{12... | collective-permute-start | bytes 208904 | tf_op jit(solution)/shard_map/ppermute | solution.py:184
  84.3 7.4 %collective-permute-start.4 = (f32[32,544]{1,0:T(8,128)S(1)}, f32[32,544]{1,0:T(8,128)S(1)}, u32[]{:S(2)}, u32[]{:S(2)}) collective-permute-start(f32[32,544]{1,0:T(8,128)S(1)} %get-tuple-element.28), channel_id=1, source_target_pairs={{0,8},{8,16},{16,24},{1,9},{9,17},{17,25},{2,10},{10,18},{18,26},{... | collective-permute-start | bytes 208904 | tf_op jit(solution)/shard_map/ppermute | solution.py:183
  89.0 3.2 %collective-permute-start.5 = (f32[32,544]{1,0:T(8,128)S(1)}, f32[32,544]{1,0:T(8,128)S(1)}, u32[]{:S(2)}, u32[]{:S(2)}) collective-permute-start(f32[32,544]{1,0:T(8,128)S(1)} %get-tuple-element.29), channel_id=1, source_target_pairs={{8,0},{16,8},{24,16},{9,1},{17,9},{25,17},{10,2},{18,10},{26,18},{... | collective-permute-start | bytes 208904 | tf_op jit(solution)/shard_map/ppermute | solution.py:184
  93.2 17.1 %collective-permute-start.6 = (f32[544,32]{1,0:T(8,128)S(1)}, f32[544,32]{1,0:T(8,128)S(1)}, u32[]{:S(2)}, u32[]{:S(2)}) collective-permute-start(f32[544,32]{1,0:T(8,128)S(1)} %pad_maximum_fusion.2), channel_id=1, source_target_pairs={{0,1},{1,2},{2,3},{3,4},{4,5},{5,6},{6,7},{8,9},{9,10},{10,11},{11... | collective-permute-start | bytes 208904 | tf_op jit(solution)/shard_map/ppermute | solution.py:183
  110.4 11.1 %collective-permute-start.7 = (f32[544,32]{1,0:T(8,128)S(1)}, f32[544,32]{1,0:T(8,128)S(1)}, u32[]{:S(2)}, u32[]{:S(2)}) collective-permute-start(f32[544,32]{1,0:T(8,128)S(1)} %get-tuple-element.17), channel_id=1, source_target_pairs={{1,0},{2,1},{3,2},{4,3},{5,4},{6,5},{7,6},{9,8},{10,9},{11,10},{12... | collective-permute-start | bytes 208904 | tf_op jit(solution)/shard_map/ppermute | solution.py:184
  121.8 1.1 copy-start
  182.5 5.3 %collective-permute-start.8 = (f32[32,544]{1,0:T(8,128)S(1)}, f32[32,544]{1,0:T(8,128)S(1)}, u32[]{:S(2)}, u32[]{:S(2)}) collective-permute-start(f32[32,544]{1,0:T(8,128)S(1)} %get-tuple-element.24), channel_id=1, source_target_pairs={{0,8},{8,16},{16,24},{1,9},{9,17},{17,25},{2,10},{10,18},{18,26},{... | collective-permute-start | bytes 208904 | tf_op jit(solution)/shard_map/ppermute | solution.py:183
  185.1 4.3 %collective-permute-start.9 = (f32[32,544]{1,0:T(8,128)S(1)}, f32[32,544]{1,0:T(8,128)S(1)}, u32[]{:S(2)}, u32[]{:S(2)}) collective-permute-start(f32[32,544]{1,0:T(8,128)S(1)} %get-tuple-element.25), channel_id=1, source_target_pairs={{8,0},{16,8},{24,16},{9,1},{17,9},{25,17},{10,2},{18,10},{26,18},{... | collective-permute-start | bytes 208904 | tf_op jit(solution)/shard_map/ppermute | solution.py:184
  190.5 16.5 %collective-permute-start.10 = (f32[544,32]{1,0:T(8,128)S(1)}, f32[544,32]{1,0:T(8,128)S(1)}, u32[]{:S(2)}, u32[]{:S(2)}) collective-permute-start(f32[544,32]{1,0:T(8,128)S(1)} %pad_maximum_fusion), channel_id=1, source_target_pairs={{0,1},{1,2},{2,3},{3,4},{4,5},{5,6},{6,7},{8,9},{9,10},{10,11},{11... | collective-permute-start | bytes 208904 | tf_op jit(solution)/shard_map/ppermute | solution.py:183
  207.1 10.6 %collective-permute-start.11 = (f32[544,32]{1,0:T(8,128)S(1)}, f32[544,32]{1,0:T(8,128)S(1)}, u32[]{:S(2)}, u32[]{:S(2)}) collective-permute-start(f32[544,32]{1,0:T(8,128)S(1)} %get-tuple-element.12), channel_id=1, source_target_pairs={{1,0},{2,1},{3,2},{4,3},{5,4},{6,5},{7,6},{9,8},{10,9},{11,10},{12... | collective-permute-start | bytes 208904 | tf_op jit(solution)/shard_map/ppermute | solution.py:184
  218.0 1.1 copy-start.1
  260.2 1.6 copy-start.2
  260.2 2.1 copy-start.3

commit v2 on v1

--- a/solution.py
+++ b/solution.py
@@ -164,12 +164,88 @@
             place(total_ref, cell, per_row, block, blur_back(image, matrix))
 
 
+def sum_kernel(axes, own_ref, out_ref, *scratch):
+    barrier = pltpu.get_barrier_semaphore()
+    peers = 0
+    for axis, size in axes:
+        me = lax.axis_index(axis)
+        for step in range(1, size):
+            pl.semaphore_signal(
+                barrier,
+                inc=1,
+                device_id={axis: lax.rem(me + step, size)},
+                device_id_type=pl.DeviceIdType.MESH,
+            )
+        peers += size - 1
+    pl.semaphore_wait(barrier, peers)
+    source = own_ref
+    for number, (axis, size) in enumerate(axes):
+        total_ref, landed, sent, received = scratch[4 * number : 4 * number + 4]
+        me = lax.axis_index(axis)
+        copies = [
+            pltpu.make_async_remote_copy(
+                src_ref=source,
+                dst_ref=landed.at[step - 1],
+                send_sem=sent.at[step - 1],
+                recv_sem=received.at[step - 1],
+                device_id={axis: lax.rem(me + step, size)},
+                device_id_type=pl.DeviceIdType.MESH,
+            )
+            for step in range(1, size)
+        ]
+        for copy in copies:
+            copy.start()
+        for copy in copies:
+            copy.wait()
+        total = source[...]
+        for step in range(size - 1):
+            total = total + landed[step]
+        total_ref[...] = total
+        source = total_ref
+    out_ref[...] = source[...]
+
+
+def sum_over_mesh(values, number):
+    axes = [(axis, lax.axis_size(axis)) for axis in ("ty", "tx")]
+    shape = (8, LANES)
+    scratch = []
+    for _, size in axes:
+        scratch += [
+            pltpu.VMEM(shape, jnp.float32),
+            pltpu.VMEM((size - 1,) + shape, jnp.float32),
+            pltpu.SemaphoreType.DMA((size - 1,)),
+            pltpu.SemaphoreType.DMA((size - 1,)),
+        ]
+    rows = jnp.pad(values, (0, shape[0] - values.shape[0]))
+    summed = pl.pallas_call(
+        functools.partial(sum_kernel, axes),
+        out_shape=jax.ShapeDtypeStruct(shape, jnp.float32),
+        in_specs=[vmem()],
+        out_specs=vmem(),
+        scratch_shapes=scratch,
+        compiler_params=pltpu.CompilerParams(collective_id=number, has_side_effects=True),
+        name="sum_mesh",
+    )(jnp.broadcast_to(rows[:, None], shape))
+    return [summed[row, 0] for row in range(values.shape[0])]
+
+
 def vmem():
     return pl.BlockSpec(memory_space=pltpu.VMEM)
 
 
 def smem():
     return pl.BlockSpec(memory_space=pltpu.SMEM)
+
+
+def flat_strip(strip):
+    count = LANES // strip.shape[1]
+    parts = strip.reshape(count, strip.shape[0] // count, strip.shape[1])
+    return jnp.concatenate([parts[i] for i in range(count)], axis=1)
+
+
+def tall_strip(flat, shape):
+    count = LANES // shape[1]
+    return jnp.concatenate([flat[:, i * shape[1] : (i + 1) * shape[1]] for i in range(count)], axis=0)
 
 
 def share_edges(value, axis, dim, width):
@@ -180,8 +256,13 @@
     first = lax.slice_in_dim(value, 0, 2 * width, axis=dim)
     middle = lax.slice_in_dim(value, 2 * width, length - 2 * width, axis=dim)
     last = lax.slice_in_dim(value, length - 2 * width, length, axis=dim)
-    before = lax.ppermute(last, axis, up)
-    after = lax.ppermute(first, axis, down)
+    if dim == 1:
+        before = lax.ppermute(flat_strip(last), axis, up)
+        after = lax.ppermute(flat_strip(first), axis, down)
+        before, after = tall_strip(before, last.shape), tall_strip(after, first.shape)
+    else:
+        before = lax.ppermute(last, axis, up)
+        after = lax.ppermute(first, axis, down)
     index = lax.broadcasted_iota(jnp.int32, first.shape, dim)
     first = jnp.where((position > 0) | (index >= width), first + before, 0.0)
     last = jnp.where((position < size - 1) | (index < width), last + after, 0.0)
@@ -261,7 +342,7 @@
             pairs = pairs + [(residual, applied), (applied, applied)]
         if norm_now is None:
             pairs = pairs + [(residual, residual)]
-        sums = lax.psum(jnp.stack(products(pairs)), ("ty", "tx"))
+        sums = sum_over_mesh(jnp.stack(products(pairs)), iteration)
         if norm_now is None:
             norm_now = sums[-1]
         step_size = norm_now / sums[0]

time: 266 us -> 185 us (0.70)
  blocking collectives: 78.1 us -> 0 us
  Pallas kernels: 25 us -> 73.5 us
  waiting for transfers between devices: 65.3 us -> 24.3 us
  starting transfers between devices: 55.5 us -> 34.7 us
  local copies, waits for them, and re-layouts: 12.9 us -> 21.6 us
    psum x2 -> x0, blocking collectives: 78.1 us -> none  [body(): sums = lax.psum(jnp.stack(products(pairs)), ('ty', 'tx'))]
    pallas_call x0 -> x2, Pallas kernels: none -> 46.2 us  [sum_over_mesh(): pl.pallas_call(functools.partial(sum_kernel, axes), out_shape=jax.ShapeDt...]
    ppermute x6 -> x3, starting transfers between devices: 40.5 us -> 6.03 us  [share_edges(): before = lax.ppermute(last, axis, up)]
    ppermute x6 -> x3, waiting for transfers between devices: 32.8 us -> 2.13 us  [share_edges(): after = lax.ppermute(first, axis, down)]
    ppermute x0 -> x6, starting transfers between devices: none -> 17.5 us  [the longest x3 13.7 us: share_edges(): before = lax.ppermute(flat_strip(last), axis, up)]
    ppermute x6 -> x3, waiting for transfers between devices: 15.2 us -> 0.01 us  [share_edges(): before = lax.ppermute(last, axis, up)]
    slice x1 -> x11, local copies, waits for them, and re-layouts: 0.65 us -> 6.31 us  [the longest x3 3.03 us: flat_strip(): return jnp.concatenate([parts[i] for i in range(count)], axis=1)]
    ppermute x0 -> x6, waiting for transfers between devices: none -> 4.89 us  [the longest x3 4.88 us: share_edges(): before = lax.ppermute(flat_strip(last), axis, up)]
  transfers between devices with their start and end apart: 13 -> 13, of which waited for: 10 -> 7; matrix products, arithmetic and copies ran while one was open for 2% -> 5% of each run, Pallas kernels for 0% -> 0%
where the time goes in v2:
time: 185 us; the launch traced here: 183 us
  Pallas kernels  73.5 us (40%)
  starting transfers between devices  34.7 us (19%)
  waiting for transfers between devices  24.3 us (13%)
  other arithmetic  23.3 us (13%)
  local copies, waits for them, and re-layouts  21.6 us (12%)
  between operations  5.61 us (3%)
    pallas_call x2, Pallas kernels, sum_over_mesh(): pl.pallas_call(functools.partial(sum_kernel, axes), out_shape=jax.ShapeDt...  46.2 us
    pallas_call x2, Pallas kernels, body(): pl.pallas_call(functools.partial(normal_kernel, slot_count, per_row, bloc...  18.6 us
    all_to_all x1, waiting for transfers between devices, body(): lax.all_to_all(packed, 'tx', split_axis=0, concat_axis=0, tiled=True)  17.3 us
    ppermute x3, starting transfers between devices, share_edges(): before = lax.ppermute(flat_strip(last), axis, up)  13.7 us
    all_to_all x1, starting transfers between devices, body(): lax.all_to_all(packed, 'tx', split_axis=0, concat_axis=0, tiled=True)  7.31 us
    pallas_call x1, Pallas kernels, body(): pl.pallas_call(functools.partial(first_kernel, slot_count, per_row, block...  6.68 us
    ppermute x3, starting transfers between devices, share_edges(): before = lax.ppermute(last, axis, up)  6.03 us
    slice x6, local copies, waits for them, and re-layouts, share_edges(): middle = lax.slice_in_dim(value, 2 * width, length - 2 * width, axis=dim)  5.16 us
  transfers between devices with their start and end apart: 13, of which 7 were waited for; matrix products, arithmetic and copies ran while one was open for 5% of the time, Pallas kernels for 0%

profile of v2, /device:TPU:0, one launch (start us, length us, event | category | flops | bytes accessed | tf_op | source)
XLA Modules:
  0.0 183.1 jit_solution(1358936172419815074)
XLA Ops:
  0.6 0.8 broadcast_subtract_fusion.1
  1.4 0.8 multiply_bitcast_fusion.1
  2.2 0.9 select_reduce_fusion.2
  3.1 0.7 multiply_add_fusion.3
  3.7 0.6 select_reduce_fusion
  4.3 0.6 convert_element_type.53.tag_ref
  4.9 1.1 reduce_sum.79
  6.0 1.0 broadcast_divide_fusion
  7.3 0.7 reshape.106.taps_ref
  8.0 2.0 %pack.1 = bf16[16,160,128]{2,1,0:T(8,128)(2,1)} custom-call(s32[16]{0:T(128)} %get-tuple-element.10.source_ref, f32[16]{0:T(128)} %convert_element_type.53.tag_ref, f32[8,128,128]{2,1,0:T(8,128)} %exposures_ref.1, bf16[8,16,128]{2,1,0:T(8,128)(2,1)} %reshape.106.taps_ref), custom_call_target="tpu_custom_call" | custom-call | tf_op jit(solution)/shard_map/pack/pallas_call | solution.py:294
  10.0 7.3 %all-to-all-start = ((bf16[16,160,128]{2,1,0:T(8,128)(2,1)}), bf16[16,160,128]{2,1,0:T(8,128)(2,1)S(1)}, u32[]{:S(2)}, u32[]{:S(2)}) async-start(bf16[16,160,128]{2,1,0:T(8,128)(2,1)} %pack.1), calls=%async_computation | async-start | bytes 1310720 | tf_op jit(solution)/shard_map/all_to_all | solution.py:301
  17.3 17.3 %all-to-all-done.frames_ref = bf16[16,160,128]{2,1,0:T(8,128)(2,1)S(1)} async-done(((bf16[16,160,128]{2,1,0:T(8,128)(2,1)}), bf16[16,160,128]{2,1,0:T(8,128)(2,1)S(1)}, u32[]{:S(2)}, u32[]{:S(2)}) %all-to-all-start) | async-done | bytes 655392 | tf_op jit(solution)/shard_map/all_to_all | solution.py:301
  34.6 0.9 fusion.28.cell_ref
  35.5 6.7 %first_adjoint.1 = (f32[544,640]{1,0:T(8,128)}, bf16[16,256,256]{2,1,0:T(8,128)(2,1)}) custom-call(s32[16]{0:T(128)} %fusion.28.cell_ref, bf16[16,160,128]{2,1,0:T(8,128)(2,1)} %copy-done.4), custom_call_target="tpu_custom_call" | custom-call | tf_op jit(solution)/shard_map/first_adjoint/pallas_call | solution.py:304
  42.2 0.9 fusion.37
  43.1 1.3 collective-permute-start
  44.4 1.3 collective-permute-start.1
  45.7 1.0 fusion.36
  46.8 1.4 slice.353
  48.1 1.2 collective-permute-done.1
  49.3 1.0 add_select_fusion.5
  50.5 1.3 collective-permute-start.3
  51.9 4.5 %collective-permute-start.2 = (f32[136,128]{1,0:T(8,128)S(1)}, f32[136,128]{1,0:T(8,128)S(1)}, u32[]{:S(2)}, u32[]{:S(2)}) collective-permute-start(f32[136,128]{1,0:T(8,128)S(1)} %get-tuple-element.42), channel_id=1, source_target_pairs={{0,1},{1,2},{2,3},{3,4},{4,5},{5,6},{6,7},{8,9},{9,10},{10,11},{11... | collective-permute-start | bytes 208904 | tf_op jit(solution)/shard_map/ppermute | solution.py:260
  57.0 2.0 %collective-permute-done.2 = f32[136,128]{1,0:T(8,128)S(1)} collective-permute-done((f32[136,128]{1,0:T(8,128)S(1)}, f32[136,128]{1,0:T(8,128)S(1)}, u32[]{:S(2)}, u32[]{:S(2)}) %collective-permute-start.2) | collective-permute-done | bytes 69664 | tf_op jit(solution)/shard_map/ppermute | solution.py:260
  59.6 0.9 pad.35.field_ref
  60.5 9.3 %normal.2 = f32[544,640]{1,0:T(8,128)} custom-call(s32[16]{0:T(128)} %fusion.28.cell_ref, bf16[544,640]{1,0:T(8,128)(2,1)} %pad.35.field_ref, bf16[16,256,256]{2,1,0:T(8,128)(2,1)} %get-tuple-element.5.matrix_ref), custom_call_target="tpu_custom_call" | custom-call | tf_op jit(solution)/shard_map/normal/pallas_call | solution.py:331
  69.8 0.9 fusion.35
  70.8 3.3 %collective-permute-start.4 = (f32[32,544]{1,0:T(8,128)S(1)}, f32[32,544]{1,0:T(8,128)S(1)}, u32[]{:S(2)}, u32[]{:S(2)}) collective-permute-start(f32[32,544]{1,0:T(8,128)S(1)} %get-tuple-element.38), channel_id=1, source_target_pairs={{0,8},{8,16},{16,24},{1,9},{9,17},{17,25},{2,10},{10,18},{18,26},{... | collective-permute-start | bytes 208904 | tf_op jit(solution)/shard_map/ppermute | solution.py:264
  74.1 1.3 collective-permute-start.5
  75.4 1.0 fusion.34
  76.4 1.4 slice.441
  78.2 1.0 add_select_fusion.3
  79.4 1.3 collective-permute-start.7
  80.8 4.5 %collective-permute-start.6 = (f32[136,128]{1,0:T(8,128)S(1)}, f32[136,128]{1,0:T(8,128)S(1)}, u32[]{:S(2)}, u32[]{:S(2)}) collective-permute-start(f32[136,128]{1,0:T(8,128)S(1)} %get-tuple-element.30), channel_id=1, source_target_pairs={{0,1},{1,2},{2,3},{3,4},{4,5},{5,6},{6,7},{8,9},{9,10},{10,11},{11... | collective-permute-start | bytes 208904 | tf_op jit(solution)/shard_map/ppermute | solution.py:260
  85.8 1.4 collective-permute-done.6
  87.5 0.5 maximum_add_fusion
  88.0 1.1 copy-done
  89.1 1.3 multiply_reduce_fusion.3
  90.4 2.0 %select_maximum_fusion.6 = f32[8]{0:T(128)S(1)} fusion(f32[1]{0:T(128)} %bitcast.5, f32[1]{0:T(128)} %bitcast.4, f32[1]{0:T(128)} %bitcast.3), kind=kLoop, calls=%fused_computation.83 | loop fusion | flops 64 | bytes 44 | tf_op jit(solution)/shard_map/stack | solution.py:345
  92.4 0.7 broadcast_in_dim.72.own_ref
  93.1 25.5 %sum_mesh.2 = f32[8,128]{1,0:T(8,128)} custom-call(f32[8,128]{1,0:T(8,128)} %broadcast_in_dim.72.own_ref), custom_call_target="tpu_custom_call" | custom-call | tf_op jit(solution)/shard_map/sum_mesh/pallas_call | solution.py:220
  118.6 1.4 fusion.44
  123.9 2.7 %fusion.30 = (bf16[544,544]{1,0:T(8,128)(2,1)S(1)}, f32[544,544]{1,0:T(8,128)S(1)}, f32[544,544]{1,0:T(8,128)}) fusion(f32[544,544]{1,0:T(8,128)S(1)} %get-tuple-element.15, f32[]{:T(128)S(6)} %div.34, f32[544,544]{1,0:T(8,128)} %copy-done, f32[]{:T(128)S(6)} %div.33), kind=kLoop, calls=%fused_computation.93 | loop fusion | flops 1479680 | bytes 5326856 | tf_op jit(solution)/shard_map/convert_element_type | solution.py:330
  126.6 0.9 pad.37.field_ref
  127.5 9.3 %normal.3 = f32[544,640]{1,0:T(8,128)} custom-call(s32[16]{0:T(128)} %fusion.28.cell_ref, bf16[544,640]{1,0:T(8,128)(2,1)} %pad.37.field_ref, bf16[16,256,256]{2,1,0:T(8,128)(2,1)} %get-tuple-element.5.matrix_ref), custom_call_target="tpu_custom_call" | custom-call | tf_op jit(solution)/shard_map/normal/pallas_call | solution.py:331
  136.8 0.9 fusion.33
  137.7 1.4 collective-permute-start.8
  139.2 1.3 collective-permute-start.9
  140.5 1.0 fusion.32
  141.5 1.4 slice.462
  142.9 0.5 collective-permute-done.9
  143.4 1.0 add_select_fusion.1
  144.6 1.3 collective-permute-start.11
  146.0 4.5 %collective-permute-start.10 = (f32[136,128]{1,0:T(8,128)S(1)}, f32[136,128]{1,0:T(8,128)S(1)}, u32[]{:S(2)}, u32[]{:S(2)}) collective-permute-start(f32[136,128]{1,0:T(8,128)S(1)} %get-tuple-element.18), channel_id=1, source_target_pairs={{0,1},{1,2},{2,3},{3,4},{4,5},{5,6},{6,7},{8,9},{9,10},{10,11},{11... | collective-permute-start | bytes 208904 | tf_op jit(solution)/shard_map/ppermute | solution.py:260
  151.0 1.4 collective-permute-done.10
  153.2 1.1 copy-done.1
  154.2 1.2 multiply_reduce_fusion
  155.5 0.6 pad.38
  156.1 0.7 broadcast_in_dim.73.own_ref
  156.8 20.7 %sum_mesh.3 = f32[8,128]{1,0:T(8,128)} custom-call(f32[8,128]{1,0:T(8,128)} %broadcast_in_dim.73.own_ref), custom_call_target="tpu_custom_call" | custom-call | tf_op jit(solution)/shard_map/sum_mesh/pallas_call | solution.py:220
  177.5 1.2 slice.426
  179.4 1.6 multiply_add_fusion.1
  180.9 0.5 copy-done.3
  181.5 1.6 slice_subtract_fusion
  (41 shorter events, 4.4 us)
Async XLA Ops:
  10.0 24.6 %all-to-all-start = ((bf16[16,160,128]{2,1,0:T(8,128)(2,1)}), bf16[16,160,128]{2,1,0:T(8,128)(2,1)S(1)}, u32[]{:S(2)}, u32[]{:S(2)}) async-start(bf16[16,160,128]{2,1,0:T(8,128)(2,1)} %pack.1), calls=%async_computation | async-start | bytes 1310720 | tf_op jit(solution)/shard_map/all_to_all | solution.py:301
  34.6 0.9 copy-start.4
  43.1 5.0 %collective-permute-start = (f32[32,544]{1,0:T(8,128)S(1)}, f32[32,544]{1,0:T(8,128)S(1)}, u32[]{:S(2)}, u32[]{:S(2)}) collective-permute-start(f32[32,544]{1,0:T(8,128)S(1)} %get-tuple-element.50), channel_id=1, source_target_pairs={{0,8},{8,16},{16,24},{1,9},{9,17},{17,25},{2,10},{10,18},{18,26},{... | collective-permute-start | bytes 208904 | tf_op jit(solution)/shard_map/ppermute | solution.py:264
  44.4 4.9 %collective-permute-start.1 = (f32[32,544]{1,0:T(8,128)S(1)}, f32[32,544]{1,0:T(8,128)S(1)}, u32[]{:S(2)}, u32[]{:S(2)}) collective-permute-start(f32[32,544]{1,0:T(8,128)S(1)} %get-tuple-element.51), channel_id=1, source_target_pairs={{8,0},{16,8},{24,16},{9,1},{17,9},{25,17},{10,2},{18,10},{26,18},{... | collective-permute-start | bytes 208904 | tf_op jit(solution)/shard_map/ppermute | solution.py:265
  50.5 6.3 %collective-permute-start.3 = (f32[136,128]{1,0:T(8,128)S(1)}, f32[136,128]{1,0:T(8,128)S(1)}, u32[]{:S(2)}, u32[]{:S(2)}) collective-permute-start(f32[136,128]{1,0:T(8,128)S(1)} %get-tuple-element.43), channel_id=1, source_target_pairs={{1,0},{2,1},{3,2},{4,3},{5,4},{6,5},{7,6},{9,8},{10,9},{11,10},{12... | collective-permute-start | bytes 208904 | tf_op jit(solution)/shard_map/ppermute | solution.py:261
  51.9 7.0 %collective-permute-start.2 = (f32[136,128]{1,0:T(8,128)S(1)}, f32[136,128]{1,0:T(8,128)S(1)}, u32[]{:S(2)}, u32[]{:S(2)}) collective-permute-start(f32[136,128]{1,0:T(8,128)S(1)} %get-tuple-element.42), channel_id=1, source_target_pairs={{0,1},{1,2},{2,3},{3,4},{4,5},{5,6},{6,7},{8,9},{9,10},{10,11},{11... | collective-permute-start | bytes 208904 | tf_op jit(solution)/shard_map/ppermute | solution.py:260
  70.8 7.0 %collective-permute-start.4 = (f32[32,544]{1,0:T(8,128)S(1)}, f32[32,544]{1,0:T(8,128)S(1)}, u32[]{:S(2)}, u32[]{:S(2)}) collective-permute-start(f32[32,544]{1,0:T(8,128)S(1)} %get-tuple-element.38), channel_id=1, source_target_pairs={{0,8},{8,16},{16,24},{1,9},{9,17},{17,25},{2,10},{10,18},{18,26},{... | collective-permute-start | bytes 208904 | tf_op jit(solution)/shard_map/ppermute | solution.py:264
  74.1 4.1 %collective-permute-start.5 = (f32[32,544]{1,0:T(8,128)S(1)}, f32[32,544]{1,0:T(8,128)S(1)}, u32[]{:S(2)}, u32[]{:S(2)}) collective-permute-start(f32[32,544]{1,0:T(8,128)S(1)} %get-tuple-element.39), channel_id=1, source_target_pairs={{8,0},{16,8},{24,16},{9,1},{17,9},{25,17},{10,2},{18,10},{26,18},{... | collective-permute-start | bytes 208904 | tf_op jit(solution)/shard_map/ppermute | solution.py:265
  79.4 6.3 %collective-permute-start.7 = (f32[136,128]{1,0:T(8,128)S(1)}, f32[136,128]{1,0:T(8,128)S(1)}, u32[]{:S(2)}, u32[]{:S(2)}) collective-permute-start(f32[136,128]{1,0:T(8,128)S(1)} %get-tuple-element.31), channel_id=1, source_target_pairs={{1,0},{2,1},{3,2},{4,3},{5,4},{6,5},{7,6},{9,8},{10,9},{11,10},{12... | collective-permute-start | bytes 208904 | tf_op jit(solution)/shard_map/ppermute | solution.py:261
  80.8 6.5 %collective-permute-start.6 = (f32[136,128]{1,0:T(8,128)S(1)}, f32[136,128]{1,0:T(8,128)S(1)}, u32[]{:S(2)}, u32[]{:S(2)}) collective-permute-start(f32[136,128]{1,0:T(8,128)S(1)} %get-tuple-element.30), channel_id=1, source_target_pairs={{0,1},{1,2},{2,3},{3,4},{4,5},{5,6},{6,7},{8,9},{9,10},{10,11},{11... | collective-permute-start | bytes 208904 | tf_op jit(solution)/shard_map/ppermute | solution.py:260
  87.9 1.1 copy-start
  137.7 5.1 %collective-permute-start.8 = (f32[32,544]{1,0:T(8,128)S(1)}, f32[32,544]{1,0:T(8,128)S(1)}, u32[]{:S(2)}, u32[]{:S(2)}) collective-permute-start(f32[32,544]{1,0:T(8,128)S(1)} %get-tuple-element.26), channel_id=1, source_target_pairs={{0,8},{8,16},{16,24},{1,9},{9,17},{17,25},{2,10},{10,18},{18,26},{... | collective-permute-start | bytes 208904 | tf_op jit(solution)/shard_map/ppermute | solution.py:264
  139.2 4.2 %collective-permute-start.9 = (f32[32,544]{1,0:T(8,128)S(1)}, f32[32,544]{1,0:T(8,128)S(1)}, u32[]{:S(2)}, u32[]{:S(2)}) collective-permute-start(f32[32,544]{1,0:T(8,128)S(1)} %get-tuple-element.27), channel_id=1, source_target_pairs={{8,0},{16,8},{24,16},{9,1},{17,9},{25,17},{10,2},{18,10},{26,18},{... | collective-permute-start | bytes 208904 | tf_op jit(solution)/shard_map/ppermute | solution.py:265
  144.6 6.3 %collective-permute-start.11 = (f32[136,128]{1,0:T(8,128)S(1)}, f32[136,128]{1,0:T(8,128)S(1)}, u32[]{:S(2)}, u32[]{:S(2)}) collective-permute-start(f32[136,128]{1,0:T(8,128)S(1)} %get-tuple-element.19), channel_id=1, source_target_pairs={{1,0},{2,1},{3,2},{4,3},{5,4},{6,5},{7,6},{9,8},{10,9},{11,10},{12... | collective-permute-start | bytes 208904 | tf_op jit(solution)/shard_map/ppermute | solution.py:261
  146.0 6.5 %collective-permute-start.10 = (f32[136,128]{1,0:T(8,128)S(1)}, f32[136,128]{1,0:T(8,128)S(1)}, u32[]{:S(2)}, u32[]{:S(2)}) collective-permute-start(f32[136,128]{1,0:T(8,128)S(1)} %get-tuple-element.18), channel_id=1, source_target_pairs={{0,1},{1,2},{2,3},{3,4},{4,5},{5,6},{6,7},{8,9},{9,10},{10,11},{11... | collective-permute-start | bytes 208904 | tf_op jit(solution)/shard_map/ppermute | solution.py:260
  153.1 1.1 copy-start.1
  179.3 1.6 copy-start.2
  179.4 2.1 %copy-start.3 = (f32[544,544]{1,0:T(8,128)S(1)}, f32[544,544]{1,0:T(8,128)}, u32[]{:S(2)}) copy-start(f32[544,544]{1,0:T(8,128)} %get-tuple-element.13) | copy-start | bytes 3551236
